TPU v7x, 16 devices: a 4x2x1 block of a 4x4x8 slice. The times are simulated.
16 devices in a mesh: dp: 2 (over y, z), cp: 8 (over x, core).
Axes of the slice: x: 4, y: 2, z: 1, core: 2. Of those that a mesh axis runs over, the one named last changes fastest.
The devices are a block of a 4x4x8 slice.
Arguments:
- queries: bfloat16 [2, 4096, 16, 256], P('dp', 'cp'), parts along dimension 0
- keys: bfloat16 [2, 4096, 8, 256], P('dp', 'cp'), parts along dimension 0
- values: bfloat16 [2, 4096, 8, 256], P('dp', 'cp'), parts along dimension 0
- out_grad: bfloat16 [2, 4096, 16, 256], P('dp', 'cp'), parts along dimension 0
Outputs:
- output 1: bfloat16 [2, 4096, 16, 256], P('dp', 'cp'), parts along dimension 0
- output 2: float32 [2, 16, 4096], P('dp', None, 'cp'), parts along dimension 0
- output 3: bfloat16 [2, 4096, 16, 256], P('dp', 'cp'), parts along dimension 0
- output 4: bfloat16 [2, 4096, 8, 256], P('dp', 'cp'), parts along dimension 0
- output 5: bfloat16 [2, 4096, 8, 256], P('dp', 'cp'), parts along dimension 0
There are 2 independent parts. A program takes and returns all parts, laid end to end along the dimension named above; each array names one.
All inputs are finite; a program needn't handle non-finite values.
Results may differ from a plain program's by a relative error of at most 0.0187391.
Values are sent between devices in bfloat16 or wider.
A program may use at most 768 MiB of HBM per device.

v0:
```python
import jax
import jax.numpy as jnp
from jax import lax
from jax.sharding import PartitionSpec as P


def block_scores(query5, key_blk, scale, causal):
    scores = jnp.einsum("bqgrd,bkgd->bgrqk", query5, key_blk, preferred_element_type=jnp.float32) * scale
    if causal:
        tokens = query5.shape[1]
        row_idx = lax.broadcasted_iota(jnp.int32, (tokens, tokens), 0)
        col_idx = lax.broadcasted_iota(jnp.int32, (tokens, tokens), 1)
        scores = jnp.where(row_idx >= col_idx, scores, -jnp.inf)
    return scores


def forward_step(query5, key_blk, value_blk, state, scale, causal):
    run_max, run_sum, run_acc = state
    scores = block_scores(query5, key_blk, scale, causal)
    new_max = jnp.maximum(run_max, jnp.max(scores, axis=-1))
    alpha = jnp.exp(run_max - new_max)
    weights = jnp.exp(scores - new_max[..., None])
    new_sum = run_sum * alpha + jnp.sum(weights, axis=-1)
    new_acc = run_acc * alpha[..., None] + jnp.einsum("bgrqk,bkgd->bgrqd", weights.astype(jnp.bfloat16), value_blk, preferred_element_type=jnp.float32)
    return new_max, new_sum, new_acc


def backward_step(query5, grad5, row_lse, delta, key_blk, value_blk, scale, causal):
    scores = block_scores(query5, key_blk, scale, causal)
    prob_mat = jnp.exp(scores - row_lse[..., None])
    grad_prob = jnp.einsum("bqgrd,bkgd->bgrqk", grad5, value_blk, preferred_element_type=jnp.float32)
    grad_score = (prob_mat * (grad_prob - delta[..., None])).astype(jnp.bfloat16)
    prob_low = prob_mat.astype(jnp.bfloat16)
    dq_part = jnp.einsum("bgrqk,bkgd->bqgrd", grad_score, key_blk, preferred_element_type=jnp.float32) * scale
    dk_part = jnp.einsum("bgrqk,bqgrd->bkgd", grad_score, query5, preferred_element_type=jnp.float32) * scale
    dv_part = jnp.einsum("bgrqk,bqgrd->bkgd", prob_low, grad5, preferred_element_type=jnp.float32)
    return dq_part, dk_part, dv_part


def solution(mesh):
    cp_size = mesh.shape["cp"]
    shift_pairs = [(source, (source + 1) % cp_size) for source in range(cp_size)]

    def attention_shard(queries, keys, values, out_grad):
        batch, tokens, heads, head_dim = queries.shape
        kv_heads = keys.shape[2]
        ratio = heads // kv_heads
        scale = head_dim ** -0.5
        cp_rank = lax.axis_index("cp")
        query5 = queries.reshape(batch, tokens, kv_heads, ratio, head_dim)
        grad5 = out_grad.reshape(batch, tokens, kv_heads, ratio, head_dim)
        stat_shape = (batch, kv_heads, ratio, tokens)
        init_state = (jnp.full(stat_shape, -jnp.inf, jnp.float32), jnp.zeros(stat_shape, jnp.float32), jnp.zeros(stat_shape + (head_dim,), jnp.float32))
        diag_state = forward_step(query5, keys, values, init_state, scale, True)

        def forward_body(step, carry):
            key_cur, value_cur, state = carry
            key_cur = lax.ppermute(key_cur, "cp", shift_pairs)
            value_cur = lax.ppermute(value_cur, "cp", shift_pairs)
            state = lax.cond(step <= cp_rank, lambda prev: forward_step(query5, key_cur, value_cur, prev, scale, False), lambda prev: prev, state)
            return key_cur, value_cur, state

        run_max, run_sum, run_acc = lax.fori_loop(1, cp_size, forward_body, (keys, values, diag_state))[2]
        out5 = (run_acc / run_sum[..., None]).astype(jnp.bfloat16)
        attn_out = jnp.transpose(out5, (0, 3, 1, 2, 4)).reshape(batch, tokens, heads, head_dim)
        row_lse = run_max + jnp.log(run_sum)
        delta = jnp.einsum("bqgrd,bgrqd->bgrq", grad5, out5, preferred_element_type=jnp.float32)

        dq_diag, dk_diag, dv_diag = backward_step(query5, grad5, row_lse, delta, keys, values, scale, True)

        def backward_body(step, carry):
            key_cur, value_cur, dk_cur, dv_cur, dq_acc = carry
            key_cur = lax.ppermute(key_cur, "cp", shift_pairs)
            value_cur = lax.ppermute(value_cur, "cp", shift_pairs)
            dk_cur = lax.ppermute(dk_cur, "cp", shift_pairs)
            dv_cur = lax.ppermute(dv_cur, "cp", shift_pairs)

            def visit(acc_in):
                dk_in, dv_in, dq_in = acc_in
                dq_part, dk_part, dv_part = backward_step(query5, grad5, row_lse, delta, key_cur, value_cur, scale, False)
                return dk_in + dk_part, dv_in + dv_part, dq_in + dq_part

            dk_cur, dv_cur, dq_acc = lax.cond(step <= cp_rank, visit, lambda acc_in: acc_in, (dk_cur, dv_cur, dq_acc))
            return key_cur, value_cur, dk_cur, dv_cur, dq_acc

        carry_out = lax.fori_loop(1, cp_size, backward_body, (keys, values, dk_diag, dv_diag, dq_diag))
        dk_home = lax.ppermute(carry_out[2], "cp", shift_pairs)
        dv_home = lax.ppermute(carry_out[3], "cp", shift_pairs)
        grad_query = carry_out[4].reshape(batch, tokens, heads, head_dim).astype(jnp.bfloat16)
        return attn_out, row_lse.reshape(batch, heads, tokens), grad_query, dk_home.astype(jnp.bfloat16), dv_home.astype(jnp.bfloat16)

    seq_spec = P("dp", "cp")
    return jax.shard_map(attention_shard, mesh=mesh, in_specs=(seq_spec, seq_spec, seq_spec, seq_spec), out_specs=(seq_spec, P("dp", None, "cp"), seq_spec, seq_spec, seq_spec), check_vma=False)
```

profile of v0, /device:TPU:112, one launch (start us, length us, event | category | flops | bytes accessed | tf_op | source)
XLA Modules:
  0.0 2173.2 jit_solution(16907894954374889898)
XLA Ops:
  45.9 551.0 %while.42 = (s32[]{:T(128)}, bf16[1,512,8,256]{3,1,2,0:T(8,128)(2,1)}, bf16[1,512,8,256]{3,1,2,0:T(8,128)(2,1)}, f32[1,8,2,512]{3,2,1,0:T(2,128)S(1)}, f32[1,8,2...) while((s32[]{:T(128)}, ...), condition=%wide.region_7.8_spmd, body=%wide.region_2.7_spmd.sunk | while | flops 4332740608 | bytes 101187872 | solution.py:63
  48.6 24.7 %collective-permute-done = bf16[1,512,8,256]{3,1,2,0:T(8,128)(2,1)} collective-permute-done((bf16[1,512,8,256]{3,1,2,0:T(8,128)(2,1)}, bf16[1,512,8,256]{3,1,2,0:T(8,128)(2,1)}, u32[]{:S(2)}, u32[]{:S(2)}) %collective-permute-start) | collective-permute-done | bytes 2097184 | tf_op jit(solution)/shard_map/while/body/eval_jaxpr/ppermute | solution.py:58
  73.3 22.5 %collective-permute-done.1 = bf16[1,512,8,256]{3,1,2,0:T(8,128)(2,1)S(1)} collective-permute-done((bf16[1,512,8,256]{3,1,2,0:T(8,128)(2,1)}, bf16[1,512,8,256]{3,1,2,0:T(8,128)(2,1)S(1)}, u32[]{:S(2)}, u32[]{:S(2)}) %collective-permute-start.1) | collective-permute-done | bytes 2097184 | tf_op jit(solution)/shard_map/while/body/eval_jaxpr/ppermute | solution.py:59
  100.1 31.3 %collective-permute-start = (bf16[1,512,8,256]{3,1,2,0:T(8,128)(2,1)}, bf16[1,512,8,256]{3,1,2,0:T(8,128)(2,1)}, u32[]{:S(2)}, u32[]{:S(2)}) collective-permute-start(bf16[1,512,8,256]{3,1,2,0:T(8,128)(2,1)} %get-tuple-element.628), channel_id=1, source_target_pairs={{0,1},{1,2},{2,3},{3,4},{4,5},{5,6},{6,7},{7,0},{8,9},{9,10},{10,1... | collective-permute-start | bytes 6291464 | tf_op jit(solution)/shard_map/while/body/eval_jaxpr/ppermute | solution.py:58
  156.0 22.5 %collective-permute-done.1 = bf16[1,512,8,256]{3,1,2,0:T(8,128)(2,1)S(1)} collective-permute-done((bf16[1,512,8,256]{3,1,2,0:T(8,128)(2,1)}, bf16[1,512,8,256]{3,1,2,0:T(8,128)(2,1)S(1)}, u32[]{:S(2)}, u32[]{:S(2)}) %collective-permute-start.1) | collective-permute-done | bytes 2097184 | tf_op jit(solution)/shard_map/while/body/eval_jaxpr/ppermute | solution.py:59
  183.7 35.5 %collective-permute-start.1 = (bf16[1,512,8,256]{3,1,2,0:T(8,128)(2,1)}, bf16[1,512,8,256]{3,1,2,0:T(8,128)(2,1)S(1)}, u32[]{:S(2)}, u32[]{:S(2)}) collective-permute-start(bf16[1,512,8,256]{3,1,2,0:T(8,128)(2,1)} %get-tuple-element.629), channel_id=1, source_target_pairs={{0,1},{1,2},{2,3},{3,4},{4,5},{5,6},{6,7},{7,0},{8,9},{9,10},{10,1... | collective-permute-start | bytes 6291464 | tf_op jit(solution)/shard_map/while/body/eval_jaxpr/ppermute | solution.py:59
  238.8 22.5 %collective-permute-done.1 = bf16[1,512,8,256]{3,1,2,0:T(8,128)(2,1)S(1)} collective-permute-done((bf16[1,512,8,256]{3,1,2,0:T(8,128)(2,1)}, bf16[1,512,8,256]{3,1,2,0:T(8,128)(2,1)S(1)}, u32[]{:S(2)}, u32[]{:S(2)}) %collective-permute-start.1) | collective-permute-done | bytes 2097184 | tf_op jit(solution)/shard_map/while/body/eval_jaxpr/ppermute | solution.py:59
  271.4 50.2 %collective-permute-done = bf16[1,512,8,256]{3,1,2,0:T(8,128)(2,1)} collective-permute-done((bf16[1,512,8,256]{3,1,2,0:T(8,128)(2,1)}, bf16[1,512,8,256]{3,1,2,0:T(8,128)(2,1)}, u32[]{:S(2)}, u32[]{:S(2)}) %collective-permute-start) | collective-permute-done | bytes 2097184 | tf_op jit(solution)/shard_map/while/body/eval_jaxpr/ppermute | solution.py:58
  321.6 22.5 %collective-permute-done.1 = bf16[1,512,8,256]{3,1,2,0:T(8,128)(2,1)S(1)} collective-permute-done((bf16[1,512,8,256]{3,1,2,0:T(8,128)(2,1)}, bf16[1,512,8,256]{3,1,2,0:T(8,128)(2,1)S(1)}, u32[]{:S(2)}, u32[]{:S(2)}) %collective-permute-start.1) | collective-permute-done | bytes 2097184 | tf_op jit(solution)/shard_map/while/body/eval_jaxpr/ppermute | solution.py:59
  348.4 55.9 %collective-permute-done = bf16[1,512,8,256]{3,1,2,0:T(8,128)(2,1)} collective-permute-done((bf16[1,512,8,256]{3,1,2,0:T(8,128)(2,1)}, bf16[1,512,8,256]{3,1,2,0:T(8,128)(2,1)}, u32[]{:S(2)}, u32[]{:S(2)}) %collective-permute-start) | collective-permute-done | bytes 2097184 | tf_op jit(solution)/shard_map/while/body/eval_jaxpr/ppermute | solution.py:58
  404.4 22.5 %collective-permute-done.1 = bf16[1,512,8,256]{3,1,2,0:T(8,128)(2,1)S(1)} collective-permute-done((bf16[1,512,8,256]{3,1,2,0:T(8,128)(2,1)}, bf16[1,512,8,256]{3,1,2,0:T(8,128)(2,1)S(1)}, u32[]{:S(2)}, u32[]{:S(2)}) %collective-permute-start.1) | collective-permute-done | bytes 2097184 | tf_op jit(solution)/shard_map/while/body/eval_jaxpr/ppermute | solution.py:59
  431.2 55.9 %collective-permute-done = bf16[1,512,8,256]{3,1,2,0:T(8,128)(2,1)} collective-permute-done((bf16[1,512,8,256]{3,1,2,0:T(8,128)(2,1)}, bf16[1,512,8,256]{3,1,2,0:T(8,128)(2,1)}, u32[]{:S(2)}, u32[]{:S(2)}) %collective-permute-start) | collective-permute-done | bytes 2097184 | tf_op jit(solution)/shard_map/while/body/eval_jaxpr/ppermute | solution.py:58
  487.2 22.5 %collective-permute-done.1 = bf16[1,512,8,256]{3,1,2,0:T(8,128)(2,1)S(1)} collective-permute-done((bf16[1,512,8,256]{3,1,2,0:T(8,128)(2,1)}, bf16[1,512,8,256]{3,1,2,0:T(8,128)(2,1)S(1)}, u32[]{:S(2)}, u32[]{:S(2)}) %collective-permute-start.1) | collective-permute-done | bytes 2097184 | tf_op jit(solution)/shard_map/while/body/eval_jaxpr/ppermute | solution.py:59
  514.0 55.9 %collective-permute-done = bf16[1,512,8,256]{3,1,2,0:T(8,128)(2,1)} collective-permute-done((bf16[1,512,8,256]{3,1,2,0:T(8,128)(2,1)}, bf16[1,512,8,256]{3,1,2,0:T(8,128)(2,1)}, u32[]{:S(2)}, u32[]{:S(2)}) %collective-permute-start) | collective-permute-done | bytes 2097184 | tf_op jit(solution)/shard_map/while/body/eval_jaxpr/ppermute | solution.py:58
  569.9 22.5 %collective-permute-done.1 = bf16[1,512,8,256]{3,1,2,0:T(8,128)(2,1)S(1)} collective-permute-done((bf16[1,512,8,256]{3,1,2,0:T(8,128)(2,1)}, bf16[1,512,8,256]{3,1,2,0:T(8,128)(2,1)S(1)}, u32[]{:S(2)}, u32[]{:S(2)}) %collective-permute-start.1) | collective-permute-done | bytes 2097184 | tf_op jit(solution)/shard_map/while/body/eval_jaxpr/ppermute | solution.py:59
  663.0 1398.1 %while.43 = (s32[]{:T(128)}, bf16[1,512,8,256]{3,1,2,0:T(8,128)(2,1)}, bf16[1,512,8,256]{3,1,2,0:T(8,128)(2,1)}, f32[1,512,8,256]{3,1,2,0:T(8,128)}, f32[1,512,8...) while((s32[]{:T(128)}, ...), condition=%wide.region_11.12_spmd, body=%wide.region_8.11_spmd.sunk | while | flops 10778312704 | bytes 224494032 | solution.py:86
  663.5 145.6 %collective-permute-done.2 = bf16[1,512,8,256]{3,1,2,0:T(8,128)(2,1)S(1)} collective-permute-done((bf16[1,512,8,256]{3,1,2,0:T(8,128)(2,1)}, bf16[1,512,8,256]{3,1,2,0:T(8,128)(2,1)S(1)}, u32[]{:S(2)}, u32[]{:S(2)}) %collective-permute-start.2) | collective-permute-done | bytes 2097184 | tf_op jit(solution)/shard_map/while/body/eval_jaxpr/ppermute | solution.py:73
  843.5 168.4 %collective-permute-done.2 = bf16[1,512,8,256]{3,1,2,0:T(8,128)(2,1)S(1)} collective-permute-done((bf16[1,512,8,256]{3,1,2,0:T(8,128)(2,1)}, bf16[1,512,8,256]{3,1,2,0:T(8,128)(2,1)S(1)}, u32[]{:S(2)}, u32[]{:S(2)}) %collective-permute-start.2) | collective-permute-done | bytes 2097184 | tf_op jit(solution)/shard_map/while/body/eval_jaxpr/ppermute | solution.py:73
  1048.9 166.0 %collective-permute-done.2 = bf16[1,512,8,256]{3,1,2,0:T(8,128)(2,1)S(1)} collective-permute-done((bf16[1,512,8,256]{3,1,2,0:T(8,128)(2,1)}, bf16[1,512,8,256]{3,1,2,0:T(8,128)(2,1)S(1)}, u32[]{:S(2)}, u32[]{:S(2)}) %collective-permute-start.2) | collective-permute-done | bytes 2097184 | tf_op jit(solution)/shard_map/while/body/eval_jaxpr/ppermute | solution.py:73
  1254.3 163.5 %collective-permute-done.2 = bf16[1,512,8,256]{3,1,2,0:T(8,128)(2,1)S(1)} collective-permute-done((bf16[1,512,8,256]{3,1,2,0:T(8,128)(2,1)}, bf16[1,512,8,256]{3,1,2,0:T(8,128)(2,1)S(1)}, u32[]{:S(2)}, u32[]{:S(2)}) %collective-permute-start.2) | collective-permute-done | bytes 2097184 | tf_op jit(solution)/shard_map/while/body/eval_jaxpr/ppermute | solution.py:73
  1459.7 161.0 %collective-permute-done.2 = bf16[1,512,8,256]{3,1,2,0:T(8,128)(2,1)S(1)} collective-permute-done((bf16[1,512,8,256]{3,1,2,0:T(8,128)(2,1)}, bf16[1,512,8,256]{3,1,2,0:T(8,128)(2,1)S(1)}, u32[]{:S(2)}, u32[]{:S(2)}) %collective-permute-start.2) | collective-permute-done | bytes 2097184 | tf_op jit(solution)/shard_map/while/body/eval_jaxpr/ppermute | solution.py:73
  1655.2 168.4 %collective-permute-done.2 = bf16[1,512,8,256]{3,1,2,0:T(8,128)(2,1)S(1)} collective-permute-done((bf16[1,512,8,256]{3,1,2,0:T(8,128)(2,1)}, bf16[1,512,8,256]{3,1,2,0:T(8,128)(2,1)S(1)}, u32[]{:S(2)}, u32[]{:S(2)}) %collective-permute-start.2) | collective-permute-done | bytes 2097184 | tf_op jit(solution)/shard_map/while/body/eval_jaxpr/ppermute | solution.py:73
  1858.1 168.4 %collective-permute-done.2 = bf16[1,512,8,256]{3,1,2,0:T(8,128)(2,1)S(1)} collective-permute-done((bf16[1,512,8,256]{3,1,2,0:T(8,128)(2,1)}, bf16[1,512,8,256]{3,1,2,0:T(8,128)(2,1)S(1)}, u32[]{:S(2)}, u32[]{:S(2)}) %collective-permute-start.2) | collective-permute-done | bytes 2097184 | tf_op jit(solution)/shard_map/while/body/eval_jaxpr/ppermute | solution.py:73
  2082.8 61.6 %collective-permute-done.6 = bf16[1,512,8,256]{3,2,1,0:T(8,128)(2,1)} collective-permute-done((bf16[1,512,8,256]{3,2,1,0:T(8,128)(2,1)S(1)}, bf16[1,512,8,256]{3,2,1,0:T(8,128)(2,1)}, u32[]{:S(2)}, u32[]{:S(2)}) %collective-permute-start.6) | collective-permute-done | bytes 2097184 | tf_op jit(solution)/shard_map/ppermute | solution.py:87
  (173 shorter events, 501.5 us)
Async XLA Ops:
  663.2 171.4 %collective-permute-start.4 = (f32[1,512,8,256]{3,1,2,0:T(8,128)}, f32[1,512,8,256]{3,1,2,0:T(8,128)}, u32[]{:S(2)}, u32[]{:S(2)}) collective-permute-start(f32[1,512,8,256]{3,1,2,0:T(8,128)} %get-tuple-element.660), channel_id=1, source_target_pairs={{0,1},{1,2},{2,3},{3,4},{4,5},{5,6},{6,7},{7,0},{8,9},{9,10},{10,1... | collective-permute-start | bytes 12582920 | tf_op jit(solution)/shard_map/while/body/eval_jaxpr/ppermute | solution.py:75
  663.2 171.3 %collective-permute-start.5 = (f32[1,512,8,256]{3,1,2,0:T(8,128)}, f32[1,512,8,256]{3,1,2,0:T(8,128)}, u32[]{:S(2)}, u32[]{:S(2)}) collective-permute-start(f32[1,512,8,256]{3,1,2,0:T(8,128)} %get-tuple-element.661), channel_id=1, source_target_pairs={{0,1},{1,2},{2,3},{3,4},{4,5},{5,6},{6,7},{7,0},{8,9},{9,10},{10,1... | collective-permute-start | bytes 12582920 | tf_op jit(solution)/shard_map/while/body/eval_jaxpr/ppermute | solution.py:76
  843.4 194.0 %collective-permute-start.4 = (f32[1,512,8,256]{3,1,2,0:T(8,128)}, f32[1,512,8,256]{3,1,2,0:T(8,128)}, u32[]{:S(2)}, u32[]{:S(2)}) collective-permute-start(f32[1,512,8,256]{3,1,2,0:T(8,128)} %get-tuple-element.660), channel_id=1, source_target_pairs={{0,1},{1,2},{2,3},{3,4},{4,5},{5,6},{6,7},{7,0},{8,9},{9,10},{10,1... | collective-permute-start | bytes 12582920 | tf_op jit(solution)/shard_map/while/body/eval_jaxpr/ppermute | solution.py:75
  843.4 194.0 %collective-permute-start.5 = (f32[1,512,8,256]{3,1,2,0:T(8,128)}, f32[1,512,8,256]{3,1,2,0:T(8,128)}, u32[]{:S(2)}, u32[]{:S(2)}) collective-permute-start(f32[1,512,8,256]{3,1,2,0:T(8,128)} %get-tuple-element.661), channel_id=1, source_target_pairs={{0,1},{1,2},{2,3},{3,4},{4,5},{5,6},{6,7},{7,0},{8,9},{9,10},{10,1... | collective-permute-start | bytes 12582920 | tf_op jit(solution)/shard_map/while/body/eval_jaxpr/ppermute | solution.py:76
  843.4 168.5 %collective-permute-start.2 = (bf16[1,512,8,256]{3,1,2,0:T(8,128)(2,1)}, bf16[1,512,8,256]{3,1,2,0:T(8,128)(2,1)S(1)}, u32[]{:S(2)}, u32[]{:S(2)}) collective-permute-start(bf16[1,512,8,256]{3,1,2,0:T(8,128)(2,1)} %get-tuple-element.658), channel_id=1, source_target_pairs={{0,1},{1,2},{2,3},{3,4},{4,5},{5,6},{6,7},{7,0},{8,9},{9,10},{10,1... | collective-permute-start | bytes 6291464 | tf_op jit(solution)/shard_map/while/body/eval_jaxpr/ppermute | solution.py:73
  843.5 191.0 %collective-permute-start.3 = (bf16[1,512,8,256]{3,1,2,0:T(8,128)(2,1)}, bf16[1,512,8,256]{3,1,2,0:T(8,128)(2,1)}, u32[]{:S(2)}, u32[]{:S(2)}) collective-permute-start(bf16[1,512,8,256]{3,1,2,0:T(8,128)(2,1)} %get-tuple-element.659), channel_id=1, source_target_pairs={{0,1},{1,2},{2,3},{3,4},{4,5},{5,6},{6,7},{7,0},{8,9},{9,10},{10,1... | collective-permute-start | bytes 6291464 | tf_op jit(solution)/shard_map/while/body/eval_jaxpr/ppermute | solution.py:74
  1046.3 194.0 %collective-permute-start.4 = (f32[1,512,8,256]{3,1,2,0:T(8,128)}, f32[1,512,8,256]{3,1,2,0:T(8,128)}, u32[]{:S(2)}, u32[]{:S(2)}) collective-permute-start(f32[1,512,8,256]{3,1,2,0:T(8,128)} %get-tuple-element.660), channel_id=1, source_target_pairs={{0,1},{1,2},{2,3},{3,4},{4,5},{5,6},{6,7},{7,0},{8,9},{9,10},{10,1... | collective-permute-start | bytes 12582920 | tf_op jit(solution)/shard_map/while/body/eval_jaxpr/ppermute | solution.py:75
  1046.3 194.0 %collective-permute-start.5 = (f32[1,512,8,256]{3,1,2,0:T(8,128)}, f32[1,512,8,256]{3,1,2,0:T(8,128)}, u32[]{:S(2)}, u32[]{:S(2)}) collective-permute-start(f32[1,512,8,256]{3,1,2,0:T(8,128)} %get-tuple-element.661), channel_id=1, source_target_pairs={{0,1},{1,2},{2,3},{3,4},{4,5},{5,6},{6,7},{7,0},{8,9},{9,10},{10,1... | collective-permute-start | bytes 12582920 | tf_op jit(solution)/shard_map/while/body/eval_jaxpr/ppermute | solution.py:76
  1046.4 191.0 %collective-permute-start.3 = (bf16[1,512,8,256]{3,1,2,0:T(8,128)(2,1)}, bf16[1,512,8,256]{3,1,2,0:T(8,128)(2,1)}, u32[]{:S(2)}, u32[]{:S(2)}) collective-permute-start(bf16[1,512,8,256]{3,1,2,0:T(8,128)(2,1)} %get-tuple-element.659), channel_id=1, source_target_pairs={{0,1},{1,2},{2,3},{3,4},{4,5},{5,6},{6,7},{7,0},{8,9},{9,10},{10,1... | collective-permute-start | bytes 6291464 | tf_op jit(solution)/shard_map/while/body/eval_jaxpr/ppermute | solution.py:74
  1249.3 194.0 %collective-permute-start.4 = (f32[1,512,8,256]{3,1,2,0:T(8,128)}, f32[1,512,8,256]{3,1,2,0:T(8,128)}, u32[]{:S(2)}, u32[]{:S(2)}) collective-permute-start(f32[1,512,8,256]{3,1,2,0:T(8,128)} %get-tuple-element.660), channel_id=1, source_target_pairs={{0,1},{1,2},{2,3},{3,4},{4,5},{5,6},{6,7},{7,0},{8,9},{9,10},{10,1... | collective-permute-start | bytes 12582920 | tf_op jit(solution)/shard_map/while/body/eval_jaxpr/ppermute | solution.py:75
  1249.3 194.0 %collective-permute-start.5 = (f32[1,512,8,256]{3,1,2,0:T(8,128)}, f32[1,512,8,256]{3,1,2,0:T(8,128)}, u32[]{:S(2)}, u32[]{:S(2)}) collective-permute-start(f32[1,512,8,256]{3,1,2,0:T(8,128)} %get-tuple-element.661), channel_id=1, source_target_pairs={{0,1},{1,2},{2,3},{3,4},{4,5},{5,6},{6,7},{7,0},{8,9},{9,10},{10,1... | collective-permute-start | bytes 12582920 | tf_op jit(solution)/shard_map/while/body/eval_jaxpr/ppermute | solution.py:76
  1249.3 168.5 %collective-permute-start.2 = (bf16[1,512,8,256]{3,1,2,0:T(8,128)(2,1)}, bf16[1,512,8,256]{3,1,2,0:T(8,128)(2,1)S(1)}, u32[]{:S(2)}, u32[]{:S(2)}) collective-permute-start(bf16[1,512,8,256]{3,1,2,0:T(8,128)(2,1)} %get-tuple-element.658), channel_id=1, source_target_pairs={{0,1},{1,2},{2,3},{3,4},{4,5},{5,6},{6,7},{7,0},{8,9},{9,10},{10,1... | collective-permute-start | bytes 6291464 | tf_op jit(solution)/shard_map/while/body/eval_jaxpr/ppermute | solution.py:73
  1251.8 188.5 %collective-permute-start.3 = (bf16[1,512,8,256]{3,1,2,0:T(8,128)(2,1)}, bf16[1,512,8,256]{3,1,2,0:T(8,128)(2,1)}, u32[]{:S(2)}, u32[]{:S(2)}) collective-permute-start(bf16[1,512,8,256]{3,1,2,0:T(8,128)(2,1)} %get-tuple-element.659), channel_id=1, source_target_pairs={{0,1},{1,2},{2,3},{3,4},{4,5},{5,6},{6,7},{7,0},{8,9},{9,10},{10,1... | collective-permute-start | bytes 6291464 | tf_op jit(solution)/shard_map/while/body/eval_jaxpr/ppermute | solution.py:74
  1452.2 194.0 %collective-permute-start.4 = (f32[1,512,8,256]{3,1,2,0:T(8,128)}, f32[1,512,8,256]{3,1,2,0:T(8,128)}, u32[]{:S(2)}, u32[]{:S(2)}) collective-permute-start(f32[1,512,8,256]{3,1,2,0:T(8,128)} %get-tuple-element.660), channel_id=1, source_target_pairs={{0,1},{1,2},{2,3},{3,4},{4,5},{5,6},{6,7},{7,0},{8,9},{9,10},{10,1... | collective-permute-start | bytes 12582920 | tf_op jit(solution)/shard_map/while/body/eval_jaxpr/ppermute | solution.py:75
  1452.2 194.0 %collective-permute-start.5 = (f32[1,512,8,256]{3,1,2,0:T(8,128)}, f32[1,512,8,256]{3,1,2,0:T(8,128)}, u32[]{:S(2)}, u32[]{:S(2)}) collective-permute-start(f32[1,512,8,256]{3,1,2,0:T(8,128)} %get-tuple-element.661), channel_id=1, source_target_pairs={{0,1},{1,2},{2,3},{3,4},{4,5},{5,6},{6,7},{7,0},{8,9},{9,10},{10,1... | collective-permute-start | bytes 12582920 | tf_op jit(solution)/shard_map/while/body/eval_jaxpr/ppermute | solution.py:76
  1452.2 168.5 %collective-permute-start.2 = (bf16[1,512,8,256]{3,1,2,0:T(8,128)(2,1)}, bf16[1,512,8,256]{3,1,2,0:T(8,128)(2,1)S(1)}, u32[]{:S(2)}, u32[]{:S(2)}) collective-permute-start(bf16[1,512,8,256]{3,1,2,0:T(8,128)(2,1)} %get-tuple-element.658), channel_id=1, source_target_pairs={{0,1},{1,2},{2,3},{3,4},{4,5},{5,6},{6,7},{7,0},{8,9},{9,10},{10,1... | collective-permute-start | bytes 6291464 | tf_op jit(solution)/shard_map/while/body/eval_jaxpr/ppermute | solution.py:73
  1452.2 191.0 %collective-permute-start.3 = (bf16[1,512,8,256]{3,1,2,0:T(8,128)(2,1)}, bf16[1,512,8,256]{3,1,2,0:T(8,128)(2,1)}, u32[]{:S(2)}, u32[]{:S(2)}) collective-permute-start(bf16[1,512,8,256]{3,1,2,0:T(8,128)(2,1)} %get-tuple-element.659), channel_id=1, source_target_pairs={{0,1},{1,2},{2,3},{3,4},{4,5},{5,6},{6,7},{7,0},{8,9},{9,10},{10,1... | collective-permute-start | bytes 6291464 | tf_op jit(solution)/shard_map/while/body/eval_jaxpr/ppermute | solution.py:74
  1655.1 194.0 %collective-permute-start.4 = (f32[1,512,8,256]{3,1,2,0:T(8,128)}, f32[1,512,8,256]{3,1,2,0:T(8,128)}, u32[]{:S(2)}, u32[]{:S(2)}) collective-permute-start(f32[1,512,8,256]{3,1,2,0:T(8,128)} %get-tuple-element.660), channel_id=1, source_target_pairs={{0,1},{1,2},{2,3},{3,4},{4,5},{5,6},{6,7},{7,0},{8,9},{9,10},{10,1... | collective-permute-start | bytes 12582920 | tf_op jit(solution)/shard_map/while/body/eval_jaxpr/ppermute | solution.py:75
  1655.1 194.0 %collective-permute-start.5 = (f32[1,512,8,256]{3,1,2,0:T(8,128)}, f32[1,512,8,256]{3,1,2,0:T(8,128)}, u32[]{:S(2)}, u32[]{:S(2)}) collective-permute-start(f32[1,512,8,256]{3,1,2,0:T(8,128)} %get-tuple-element.661), channel_id=1, source_target_pairs={{0,1},{1,2},{2,3},{3,4},{4,5},{5,6},{6,7},{7,0},{8,9},{9,10},{10,1... | collective-permute-start | bytes 12582920 | tf_op jit(solution)/shard_map/while/body/eval_jaxpr/ppermute | solution.py:76
  1655.1 168.5 %collective-permute-start.2 = (bf16[1,512,8,256]{3,1,2,0:T(8,128)(2,1)}, bf16[1,512,8,256]{3,1,2,0:T(8,128)(2,1)S(1)}, u32[]{:S(2)}, u32[]{:S(2)}) collective-permute-start(bf16[1,512,8,256]{3,1,2,0:T(8,128)(2,1)} %get-tuple-element.658), channel_id=1, source_target_pairs={{0,1},{1,2},{2,3},{3,4},{4,5},{5,6},{6,7},{7,0},{8,9},{9,10},{10,1... | collective-permute-start | bytes 6291464 | tf_op jit(solution)/shard_map/while/body/eval_jaxpr/ppermute | solution.py:73
  1655.1 191.0 %collective-permute-start.3 = (bf16[1,512,8,256]{3,1,2,0:T(8,128)(2,1)}, bf16[1,512,8,256]{3,1,2,0:T(8,128)(2,1)}, u32[]{:S(2)}, u32[]{:S(2)}) collective-permute-start(bf16[1,512,8,256]{3,1,2,0:T(8,128)(2,1)} %get-tuple-element.659), channel_id=1, source_target_pairs={{0,1},{1,2},{2,3},{3,4},{4,5},{5,6},{6,7},{7,0},{8,9},{9,10},{10,1... | collective-permute-start | bytes 6291464 | tf_op jit(solution)/shard_map/while/body/eval_jaxpr/ppermute | solution.py:74
  1858.0 194.0 %collective-permute-start.4 = (f32[1,512,8,256]{3,1,2,0:T(8,128)}, f32[1,512,8,256]{3,1,2,0:T(8,128)}, u32[]{:S(2)}, u32[]{:S(2)}) collective-permute-start(f32[1,512,8,256]{3,1,2,0:T(8,128)} %get-tuple-element.660), channel_id=1, source_target_pairs={{0,1},{1,2},{2,3},{3,4},{4,5},{5,6},{6,7},{7,0},{8,9},{9,10},{10,1... | collective-permute-start | bytes 12582920 | tf_op jit(solution)/shard_map/while/body/eval_jaxpr/ppermute | solution.py:75
  1858.0 194.0 %collective-permute-start.5 = (f32[1,512,8,256]{3,1,2,0:T(8,128)}, f32[1,512,8,256]{3,1,2,0:T(8,128)}, u32[]{:S(2)}, u32[]{:S(2)}) collective-permute-start(f32[1,512,8,256]{3,1,2,0:T(8,128)} %get-tuple-element.661), channel_id=1, source_target_pairs={{0,1},{1,2},{2,3},{3,4},{4,5},{5,6},{6,7},{7,0},{8,9},{9,10},{10,1... | collective-permute-start | bytes 12582920 | tf_op jit(solution)/shard_map/while/body/eval_jaxpr/ppermute | solution.py:76
  1858.0 191.0 %collective-permute-start.3 = (bf16[1,512,8,256]{3,1,2,0:T(8,128)(2,1)}, bf16[1,512,8,256]{3,1,2,0:T(8,128)(2,1)}, u32[]{:S(2)}, u32[]{:S(2)}) collective-permute-start(bf16[1,512,8,256]{3,1,2,0:T(8,128)(2,1)} %get-tuple-element.659), channel_id=1, source_target_pairs={{0,1},{1,2},{2,3},{3,4},{4,5},{5,6},{6,7},{7,0},{8,9},{9,10},{10,1... | collective-permute-start | bytes 6291464 | tf_op jit(solution)/shard_map/while/body/eval_jaxpr/ppermute | solution.py:74
  (31 other events, 1751.3 us)
where the time goes:
time: 2180 us; the launch traced here: 2170 us
  waiting for transfers between devices  1820 us (83%)
  local copies, waits for them, and re-layouts  172 us (8%)
  starting transfers between devices  93.9 us (4%)
  matrix products  62.9 us (3%)
  other arithmetic  26.6 us (1%)
    ppermute x7, waiting for transfers between devices, backward_body(): key_cur = lax.ppermute(key_cur, 'cp', shift_pairs)  1140 us
    ppermute x7, waiting for transfers between devices, forward_body(): key_cur = lax.ppermute(key_cur, 'cp', shift_pairs)  284 us
    ppermute x7, waiting for transfers between devices, forward_body(): value_cur = lax.ppermute(value_cur, 'cp', shift_pairs)  157 us
    ppermute x7, waiting for transfers between devices, backward_body(): value_cur = lax.ppermute(value_cur, 'cp', shift_pairs)  148 us
    while x42, local copies, waits for them, and re-layouts  123 us
    ppermute x1, waiting for transfers between devices, attention_shard(): dk_home = lax.ppermute(carry_out[2], 'cp', shift_pairs)  61.6 us
  transfers between devices with their start and end apart: 44, of which 30 were waited for; matrix products, arithmetic and copies ran while one was open for 2% of the time, Pallas kernels for 0%

commit v1 on v0

v1 whole, which is shorter than its diff:
```python
import functools

import jax
import jax.numpy as jnp
from jax import lax
from jax.experimental import pallas as pl
from jax.experimental.pallas import tpu as pltpu
from jax.sharding import PartitionSpec as P

MESH = pl.DeviceIdType.MESH
F32 = jnp.float32
BF16 = jnp.bfloat16


def dot_nt(lhs, rhs):
    return lax.dot_general(lhs, rhs, (((1,), (1,)), ((), ())), preferred_element_type=F32)


def dot_nn(lhs, rhs):
    return lax.dot_general(lhs, rhs, (((1,), (0,)), ((), ())), preferred_element_type=F32)


def attention_kernel(n, ratio, scale,
                     q_in, k_in, v_in, g_in,
                     o_out, l_out, dq_out, dk_out, dv_out,
                     q_all, k_all, v_all, g_all, kt_all, vt_all,
                     o_send, l_send, dq_send, dk_send, dv_send,
                     d_row, acc, dk_acc, dv_acc,
                     in_send, in_recv, out_send, out_recv, own_sem):
    me = lax.axis_index("cp")
    tokens = k_in.shape[1]
    cols = ratio * tokens

    def peer(shift):
        return lax.rem(me + shift + n, n)

    barrier = pltpu.get_barrier_semaphore()
    for shift in range(1, n):
        pl.semaphore_signal(barrier, inc=1, device_id={"cp": peer(shift)}, device_id_type=MESH)
    pl.semaphore_wait(barrier, n - 1)

    arrivals = ((k_in, k_all), (v_in, v_all), (q_in, q_all), (g_in, g_all))

    def in_copy(which, dest, source):
        src, dst = arrivals[which]
        return pltpu.make_async_remote_copy(
            src_ref=src.at[dest], dst_ref=dst.at[source],
            send_sem=in_send.at[which, dest], recv_sem=in_recv.at[which, source],
            device_id={"cp": dest}, device_id_type=MESH)

    def own_copy(which):
        src, dst = arrivals[which]
        return pltpu.make_async_copy(src.at[me], dst.at[me], own_sem.at[which])

    for which in range(4):
        own_copy(which).start()
        for shift in range(1, n):
            in_copy(which, peer(-shift), me).start()

    departures = ((o_send, o_out), (l_send, l_out), (dq_send, dq_out), (dk_send, dk_out), (dv_send, dv_out))

    def out_copy(which, dest, source):
        src, dst = departures[which]
        return pltpu.make_async_remote_copy(
            src_ref=src.at[dest], dst_ref=dst.at[source],
            send_sem=out_send.at[which, dest], recv_sem=out_recv.at[which, source],
            device_id={"cp": dest}, device_id_type=MESH)

    def home_copy(which):
        src, dst = departures[which]
        return pltpu.make_async_copy(src.at[me], dst.at[me], own_sem.at[4 + which])

    def ship(which, shift, dest):
        @pl.when(shift == 0)
        def _():
            home_copy(which).start()

        @pl.when(shift != 0)
        def _():
            out_copy(which, dest, me).start()

    def arrive(which, shift, source):
        @pl.when(shift == 0)
        def _():
            own_copy(which).wait()

        @pl.when(shift != 0)
        def _():
            in_copy(which, source, source).wait_recv()

    def prepare(shift, carry):
        source = peer(shift)
        arrive(0, shift, source)
        kt_all[source] = k_all[source].T
        arrive(1, shift, source)
        vt_all[source] = v_all[source].T
        dk_acc[source] = jnp.zeros(dk_acc.shape[1:], F32)
        dv_acc[source] = jnp.zeros(dv_acc.shape[1:], F32)
        return carry

    lax.fori_loop(0, n, prepare, 0)

    def scores(i, j, causal):
        out = dot_nt(k_all[j], q_all[i]) * scale
        if causal:
            key_idx = lax.broadcasted_iota(jnp.int32, out.shape, 0)
            query_idx = lax.rem(lax.broadcasted_iota(jnp.int32, out.shape, 1), tokens)
            out = jnp.where(key_idx <= query_idx, out, -jnp.inf)
        return out

    def forward_row(shift, carry):
        i = peer(shift)
        arrive(2, shift, i)
        first = scores(i, i, True)
        row_max = jnp.max(first, axis=0, keepdims=True)
        weights = jnp.exp(first - row_max)
        row_sum = jnp.sum(weights, axis=0, keepdims=True)
        acc[...] = dot_nn(vt_all[i], weights.astype(BF16))

        def visit(j, state):
            run_max, run_sum = state
            block = scores(i, j, False)
            new_max = jnp.maximum(run_max, jnp.max(block, axis=0, keepdims=True))
            alpha = jnp.exp(run_max - new_max)
            weights = jnp.exp(block - new_max)
            acc[...] = acc[...] * alpha + dot_nn(vt_all[j], weights.astype(BF16))
            return new_max, run_sum * alpha + jnp.sum(weights, axis=0, keepdims=True)

        row_max, row_sum = lax.fori_loop(0, i, visit, (row_max, row_sum))
        o_send[i] = (acc[...] / row_sum).T.astype(BF16)
        l_send[i] = row_max + jnp.log(row_sum)
        ship(0, shift, i)
        ship(1, shift, i)
        return carry

    lax.fori_loop(0, n, forward_row, 0)

    def backward_row(shift, carry):
        i = peer(shift)
        arrive(3, shift, i)
        d_row[...] = jnp.sum((g_all[i].astype(F32) * o_send[i].astype(F32)).T, axis=0, keepdims=True)
        acc[...] = jnp.zeros(acc.shape, F32)

        def block_grads(j, causal):
            prob = jnp.exp(scores(i, j, causal) - l_send[i])
            grad_prob = dot_nt(v_all[j], g_all[i])
            grad_score = (prob * (grad_prob - d_row[...])).astype(BF16)
            dv_acc[j] += dot_nn(prob.astype(BF16), g_all[i])
            dk_acc[j] += dot_nn(grad_score, q_all[i])
            acc[...] += dot_nn(kt_all[j], grad_score)

        block_grads(i, True)

        def visit(j, inner):
            block_grads(j, False)
            return inner

        lax.fori_loop(0, i, visit, 0)
        dq_send[i] = (acc[...] * scale).T.astype(BF16)
        ship(2, shift, i)
        return carry

    lax.fori_loop(0, n, backward_row, 0)

    def finish(shift, carry):
        j = peer(shift)
        dk_send[j] = (dk_acc[j] * scale).astype(BF16)
        ship(3, shift, j)
        dv_send[j] = dv_acc[j].astype(BF16)
        ship(4, shift, j)
        return carry

    lax.fori_loop(0, n, finish, 0)

    for which in range(4):
        for shift in range(1, n):
            in_copy(which, peer(-shift), me).wait_send()
    for which in range(5):
        home_copy(which).wait()
        for shift in range(1, n):
            out_copy(which, peer(shift), me).wait_send()
            out_copy(which, peer(-shift), peer(-shift)).wait_recv()


def solution(mesh):
    n = mesh.shape["cp"]

    def attention_shard(queries, keys, values, out_grad):
        batch, tokens, heads, head_dim = queries.shape
        kv_heads = keys.shape[2]
        ratio = heads // kv_heads
        scale = head_dim ** -0.5
        cols = ratio * tokens

        def by_head(array):
            return jnp.transpose(array[0], (1, 0, 2)).reshape(n, -1, head_dim)

        q_shape, kv_shape = (n, cols, head_dim), (n, tokens, head_dim)
        hbm = pl.BlockSpec(memory_space=pl.ANY)
        flops = 7 * 2 * cols * tokens * head_dim * n * (n + 1) // 2
        o_out, l_out, dq_out, dk_out, dv_out = pl.pallas_call(
            functools.partial(attention_kernel, n, ratio, scale),
            out_shape=(
                jax.ShapeDtypeStruct(q_shape, BF16),
                jax.ShapeDtypeStruct((n, 1, cols), F32),
                jax.ShapeDtypeStruct(q_shape, BF16),
                jax.ShapeDtypeStruct(kv_shape, BF16),
                jax.ShapeDtypeStruct(kv_shape, BF16),
            ),
            in_specs=[hbm] * 4,
            out_specs=[hbm] * 5,
            scratch_shapes=[
                pltpu.VMEM(q_shape, BF16),
                pltpu.VMEM(kv_shape, BF16),
                pltpu.VMEM(kv_shape, BF16),
                pltpu.VMEM(q_shape, BF16),
                pltpu.VMEM((n, head_dim, tokens), BF16),
                pltpu.VMEM((n, head_dim, tokens), BF16),
                pltpu.VMEM(q_shape, BF16),
                pltpu.VMEM((n, 1, cols), F32),
                pltpu.VMEM(q_shape, BF16),
                pltpu.VMEM(kv_shape, BF16),
                pltpu.VMEM(kv_shape, BF16),
                pltpu.VMEM((1, cols), F32),
                pltpu.VMEM((head_dim, cols), F32),
                pltpu.VMEM(kv_shape, F32),
                pltpu.VMEM(kv_shape, F32),
                pltpu.SemaphoreType.DMA((4, n)),
                pltpu.SemaphoreType.DMA((4, n)),
                pltpu.SemaphoreType.DMA((5, n)),
                pltpu.SemaphoreType.DMA((5, n)),
                pltpu.SemaphoreType.DMA((9,)),
            ],
            compiler_params=pltpu.CompilerParams(
                collective_id=0, has_side_effects=True, vmem_limit_bytes=67043328
            ),
            cost_estimate=pl.CostEstimate(flops=flops, bytes_accessed=24 * cols * tokens, transcendentals=0),
        )(by_head(queries), by_head(keys), by_head(values), by_head(out_grad))

        def by_token(array, count):
            return jnp.transpose(array.reshape(count, tokens, head_dim), (1, 0, 2))[None]

        return (by_token(o_out, heads), l_out.reshape(batch, heads, tokens), by_token(dq_out, heads),
                by_token(dk_out, kv_heads), by_token(dv_out, kv_heads))

    seq_spec = P("dp", "cp")
    return jax.shard_map(attention_shard, mesh=mesh, in_specs=(seq_spec, seq_spec, seq_spec, seq_spec), out_specs=(seq_spec, P("dp", None, "cp"), seq_spec, seq_spec, seq_spec), check_vma=False)
```

time: 2180 us -> 308 us (0.14)
  waiting for transfers between devices: 1820 us -> 0 us
  Pallas kernels: 0 us -> 277 us
  local copies, waits for them, and re-layouts: 172 us -> 29.1 us
  starting transfers between devices: 93.9 us -> 0 us
  matrix products: 62.9 us -> 0 us
  other arithmetic: 26.6 us -> 0.07 us
    ppermute x44 -> x0, waiting for transfers between devices: 1820 us -> none  [the longest x7 1140 us: backward_body(): key_cur = lax.ppermute(key_cur, 'cp', shift_pairs)]
    pallas_call x0 -> x1, Pallas kernels: none -> 277 us  [attention_shard(): pl.pallas_call(functools.partial(attention_kernel, n, ratio, scale), out_...]
    while x46 -> x0, local copies, waits for them, and re-layouts: 134 us -> none
    ppermute x44 -> x0, starting transfers between devices: 93.9 us -> none  [the longest x7 42.9 us: forward_body(): value_cur = lax.ppermute(value_cur, 'cp', shift_pairs)]
    dot_general x6 -> x0, matrix products: 62.9 us -> none  [the longest x1 14.8 us: backward_step(): jnp.einsum('bqgrd,bkgd->bgrqk', grad5, value_blk, preferred_element_type=...]
  transfers between devices with their start and end apart: 44 -> 0, of which waited for: 30 -> 0; matrix products, arithmetic and copies ran while one was open for 2% -> 0% of each run, Pallas kernels for 0% -> 0%
where the time goes in v1:
time: 308 us; the launch traced here: 306 us
  Pallas kernels  277 us (90%)
  local copies, waits for them, and re-layouts  29.1 us (9%)
    pallas_call x1, Pallas kernels, attention_shard(): pl.pallas_call(functools.partial(attention_kernel, n, ratio, scale), out_...  277 us
    transpose x3, local copies, waits for them, and re-layouts, by_head(): return jnp.transpose(array[0], (1, 0, 2)).reshape(n, -1, head_dim)  12.3 us
    reshape x2, local copies, waits for them, and re-layouts, by_token(): array.reshape(count, tokens, head_dim)  11.2 us

profile of v1, /device:TPU:112, one launch (start us, length us, event | category | flops | bytes accessed | tf_op | source)
XLA Modules:
  0.0 306.3 jit_solution(8584174037218417603)
XLA Ops:
  0.6 0.0 copy-start
  0.6 5.8 %copy.9 = bf16[16,512,256]{2,1,0:T(8,128)(2,1)} copy(bf16[16,512,256]{2,0,1:T(8,128)(2,1)} %bitcast.34) | data formatting | bytes 8388608 | tf_op jit(solution)/shard_map/transpose | solution.py:196
  6.5 0.0 copy-done
  6.5 0.0 copy-start.4
  6.5 0.0 copy-start.5
  6.5 3.5 %copy.12 = bf16[16,512,256]{2,1,0:T(8,128)(2,1)} copy(bf16[16,512,256]{2,0,1:T(8,128)(2,1)S(1)} %bitcast.35) | data formatting | bytes 8388608 | tf_op jit(solution)/shard_map/transpose | solution.py:196
  10.0 0.0 copy-done.4
  10.0 0.0 copy-done.5
  10.0 2.9 copy_bitcast_fusion.2
  12.9 276.5 %shard_map.83 = (bf16[8,1024,256]{2,1,0:T(8,128)(2,1)}, f32[8,1,1024]{2,1,0:T(1,128)}, bf16[8,1024,256]{2,1,0:T(8,128)(2,1)}, bf16[8,512,256]{2,1,0:T(8,128)(2,1)}, bf16[8,512,256]{2,1,0:T(8,128)(2,1)}) custom-call(bf16[8,1024,256]{2,1,0:T(8,128)(2,1)} %bitcast.38, bf16[8,512,256]{2,1,0:T(8,128)(2,1)} %get-tuple-element.21.k_in, ...), custom_call_target="tpu_custom_call" | custom-call | flops 67645734912 | bytes 12582912 | tf_op jit(solution)/shard_map/pallas_call | solution.py:201
  289.5 0.0 copy-start.6
  289.5 0.0 copy-start.3
  289.5 6.7 %copy.22 = bf16[16,512,256]{2,0,1:T(8,128)(2,1)} copy(bf16[16,512,256]{2,1,0:T(8,128)(2,1)} %bitcast.40) | data formatting | bytes 8388608 | tf_op jit(solution)/shard_map/reshape | solution.py:241
  296.2 0.0 copy-done.6
  296.2 0.1 reduce
  296.3 0.6 reshape.28
  296.9 0.0 copy-done.3
  296.9 0.0 copy-start.2
  296.9 2.5 copy.15
  299.4 0.0 copy-done.2
  299.4 0.0 copy-start.1
  299.4 2.5 copy.16
  301.9 0.0 copy-done.1
  301.9 4.4 %copy.21 = bf16[16,512,256]{2,0,1:T(8,128)(2,1)} copy(bf16[16,512,256]{2,1,0:T(8,128)(2,1)S(1)} %bitcast.36) | data formatting | bytes 8388608 | tf_op jit(solution)/shard_map/reshape | solution.py:241
Async XLA Ops:
  0.6 5.8 %copy-start = (bf16[1,512,16,256]{3,2,1,0:T(8,128)(2,1)S(1)}, bf16[1,512,16,256]{3,2,1,0:T(8,128)(2,1)}, u32[]{:S(2)}) copy-start(bf16[1,512,16,256]{3,2,1,0:T(8,128)(2,1)} %param.7) | copy-start | bytes 12582916
  6.5 3.5 %copy-start.4 = (bf16[1,512,8,256]{3,2,1,0:T(8,128)(2,1)S(1)}, bf16[1,512,8,256]{3,2,1,0:T(8,128)(2,1)}, u32[]{:S(2)}) copy-start(bf16[1,512,8,256]{3,2,1,0:T(8,128)(2,1)} %param.6) | copy-start | bytes 6291460
  6.5 3.5 %copy-start.5 = (bf16[1,512,8,256]{3,2,1,0:T(8,128)(2,1)S(1)}, bf16[1,512,8,256]{3,2,1,0:T(8,128)(2,1)}, u32[]{:S(2)}) copy-start(bf16[1,512,8,256]{3,2,1,0:T(8,128)(2,1)} %param.5) | copy-start | bytes 6291460
  289.5 6.7 %copy-start.6 = (f32[8,1,1024]{2,1,0:T(1,128)S(1)}, f32[8,1,1024]{2,1,0:T(1,128)}, u32[]{:S(2)}) copy-start(f32[8,1,1024]{2,1,0:T(1,128)} %get-tuple-element.11) | copy-start | bytes 98308
  289.5 7.4 %copy-start.3 = (bf16[8,512,256]{2,1,0:T(8,128)(2,1)S(1)}, bf16[8,512,256]{2,1,0:T(8,128)(2,1)}, u32[]{:S(2)}) copy-start(bf16[8,512,256]{2,1,0:T(8,128)(2,1)} %get-tuple-element.13) | copy-start | bytes 6291460
  296.9 2.5 copy-start.2
  299.4 2.5 copy-start.1
